TPU v7x, 32 devices: a whole 2x2x4 slice. The times are simulated.
32 devices in a mesh: wave: 4 (over y, x), freq: 8 (over z, core).
Axes of the slice: x: 2, y: 2, z: 4, core: 2. Of those that a mesh axis runs over, the one named last changes fastest.
Arguments:
- waveforms: float32 [1024, 16384], P('wave', 'freq'), may hold values from -6 to 6
- pivots: int32 [2, 128], replicated, may hold values from 0 to 1023, as said below
- nodes: int32 [1024], replicated, may hold values from 0 to 16383, as said below
Outputs:
- residual: float32 [1024, 16384], P('wave', 'freq')
- basis_rows: float32 [256, 16384], P(None, 'freq')
- fitted: float32 [1024, 16384], P('wave', 'freq')
Inputs may be any that keep to these rules, and one draw needn't show every extreme that they name: `pivots`: all 256 pivot indices are different. `nodes`: all node indices are different.
All inputs are finite; a program needn't handle non-finite values.
Results may differ from a plain program's by a relative error of at most 0.0001.
Values sent between devices are 32-bit elements; how exact they have to be, the bound alone decides.
A program may use at most 64 MiB of HBM per device.

v0:
```python
import jax
import jax.numpy as jnp
from jax import lax
from jax.sharding import PartitionSpec as P

HIGH = lax.Precision.HIGH


def body(waveforms, pivots, nodes):
    rows_here, cols_here = waveforms.shape
    row_start = lax.axis_index("wave") * rows_here
    col_start = lax.axis_index("freq") * cols_here
    picks = pivots.reshape(-1)
    count = picks.shape[0]
    local_rows = picks - row_start
    inside = ((local_rows >= 0) & (local_rows < rows_here)).astype(jnp.float32)
    picked = jnp.take(waveforms, jnp.clip(local_rows, 0, rows_here - 1), axis=0) * inside[:, None]
    pivot_rows = lax.psum(picked, "wave")
    columns = col_start + jnp.arange(cols_here, dtype=jnp.int32)
    node_count = jnp.sum((nodes[:, None] == columns[None, :]).astype(jnp.float32), axis=0)
    weighted = pivot_rows * node_count[None, :]
    left = jnp.concatenate([pivot_rows, waveforms], axis=0)
    right = jnp.concatenate([pivot_rows, weighted], axis=0)
    total = lax.psum(jnp.dot(left, right.T, precision=HIGH), "freq")
    gram, node_gram = (total[:count, :count], total[:count, count:])
    cross, node_cross = (total[count:, :count], total[count:, count:])
    factors = jnp.linalg.cholesky(jnp.stack([gram, node_gram]))
    eye = jnp.broadcast_to(jnp.eye(count, dtype=jnp.float32), factors.shape)
    inverses = jax.scipy.linalg.solve_triangular(factors, eye, lower=True)
    hi = lax.Precision.HIGHEST
    basis_rows = jnp.dot(inverses[0], pivot_rows, precision=HIGH)
    coeffs = jnp.dot(cross, inverses[0].T, precision=hi)
    residual = waveforms - jnp.dot(coeffs, basis_rows, precision=HIGH)
    coefficients = jnp.dot(
        jnp.dot(node_cross, inverses[1].T, precision=hi), inverses[1], precision=hi
    )
    fitted = jnp.dot(coefficients, pivot_rows, precision=HIGH)
    return (residual, basis_rows, fitted)


def solution(mesh):
    in_specs = (P("wave", "freq"), P(), P())
    out_specs = (P("wave", "freq"), P(None, "freq"), P("wave", "freq"))
    return jax.shard_map(body, mesh=mesh, in_specs=in_specs, out_specs=out_specs, check_vma=False)
```

profile of v0, /device:TPU:0, one launch (start us, length us, event | category | flops | bytes accessed | tf_op | source)
XLA Modules:
  0.0 288.0 jit_solution(7392579073697744297)
XLA Ops:
  7.9 0.7 compare_and_fusion
  8.6 4.0 %gather_fusion = f32[256,2048]{1,0:T(8,128)S(1)} fusion(f32[256,2048]{1,0:T(8,128)} %param.3, s32[1024]{0:T(1024)S(1)} %pad_clamp_fusion), kind=kCustom, calls=%fused_computation | custom fusion | bytes 4195328 | tf_op jit(solution)/shard_map/jit(_take)/gather | solution.py:17
  12.6 1.6 select_multiply_fusion
  14.9 0.9 convert_reduce_fusion
  15.8 70.8 %all-reduce.4.cloned.1.call-done = f32[256,2048]{1,0:T(8,128)} async-done(((f32[256,2048]{1,0:T(8,128)}), f32[256,2048]{1,0:T(8,128)}) %all-reduce.4.cloned.1.call-update) | async-done | bytes 2097168 | tf_op jit(solution)/shard_map/psum | solution.py:18
  86.6 2.0 broadcast_multiply_fusion
  88.8 4.6 %fusion = f32[512,512]{0,1:T(8,128)} fusion(f32[256,2048]{1,0:T(8,128)S(1)} %copy-done.1, f32[256,2048]{1,0:T(8,128)S(1)} %copy-done, f32[256,2048]{1,0:T(8,128)S(1)} %broadcast_multiply_fusion), kind=kOutput, calls=%fused_computation.6 | convolution fusion | flops 3223322624 | bytes 7340032 | tf_op jit(solution)/shard_map/dot_general | solution.py:24
  93.5 59.4 %all-reduce.6.cloned.1.call-done = f32[512,512]{0,1:T(8,128)} async-done(((f32[512,512]{0,1:T(8,128)}), f32[512,512]{0,1:T(8,128)}) %all-reduce.6.cloned.1.call-update) | async-done | bytes 1048592 | tf_op jit(solution)/shard_map/psum | solution.py:24
  152.9 1.1 slice_bitcast_fusion.1
  153.9 0.8 pad_maximum_fusion.4
  154.8 1.2 copy.14
  156.1 0.8 copy-done.4
  156.9 23.6 %custom-call.17 = f32[2,128,128]{2,1,0:T(8,128)S(1)} custom-call(f32[2,128,128]{2,1,0:T(8,128)S(1)} %cholesky.122), custom_call_target="Cholesky" | custom-call | tf_op jit(solution)/shard_map/jit(cholesky)/cholesky | solution.py:27
  180.6 19.7 %custom-call.18 = f32[2,1,128,128]{2,3,1,0:T(8,128)S(1)} custom-call(f32[2,1,128,128]{3,2,1,0:T(8,128)S(1)} %select_bitcast_fusion), custom_call_target="InvertDiagBlocksLowerTriangular" | custom-call | tf_op jit(solution)/shard_map/jit(cholesky)/cholesky | solution.py:27
  200.3 1.2 constant_dynamic-update-slice_fusion.1
  201.5 1.3 convolution_subtract_fusion.2
  202.8 23.5 %custom-call.19 = f32[2,128,128]{2,1,0:T(8,128)S(1)} custom-call(f32[2,128,128]{2,1,0:T(8,128)S(1)} %convolution_subtract_fusion.2), custom_call_target="Cholesky" | custom-call | tf_op jit(solution)/shard_map/jit(cholesky)/cholesky | solution.py:27
  226.7 5.3 %while.1 = (s32[]{:T(128)}, f32[2,256,256]{2,1,0:T(8,128)S(1)}, s32[2,2]{1,0:T(2,128)S(1)}, f32[2,2,128,128]{3,2,0,1:T(8,128)}, s32[]{:T(128)}) while((s32[]{:T(128)}, f32[2,256,256]{2,1,0:T(8,128)S(1)}, s32[2,2]{1,0:T(2,128)S(1)}, f32[2,2,128,128]{3,2,0,1:T(8,128)}, s32[]{:T(128)}) %tuple.30), condition=%wide.while_cond, body=%wide.while_body.sunk | while | flops 2 | bytes 263277 | solution.py:29
  227.3 2.0 bitcast_dynamic-update-slice_fusion.2
  229.9 2.0 bitcast_dynamic-update-slice_fusion.2
  231.9 40.1 %custom-call.20 = f32[2,2,128,128]{2,3,1,0:T(8,128)S(1)} custom-call(f32[2,2,128,128]{3,2,1,0:T(8,128)} %bitcast.62), custom_call_target="InvertDiagBlocksLowerTriangular" | custom-call | tf_op jit(solution)/shard_map/jit(_solve_triangular)/vmap()/triangular_solve | solution.py:29
  274.9 1.2 fusion.22
  276.1 2.5 convolution_subtract_fusion
  278.7 2.5 fusion.33
  (47 shorter events, 6.2 us)
Async XLA Ops:
  7.2 79.4 %all-reduce.4.cloned.1.call-start = ((), (), s32[]{:S(2)}) async-start(), calls=%async_computation | async-start | bytes 4194304 | tf_op jit(solution)/shard_map/psum | solution.py:18
  14.2 0.7 copy-start.6
  14.2 138.6 %all-reduce.6.cloned.1.call-start = ((), (), s32[]{:S(2)}) async-start(), calls=%async_computation.1 | async-start | bytes 2097152 | tf_op jit(solution)/shard_map/psum | solution.py:24
  15.8 72.8 %copy-start = (f32[256,2048]{1,0:T(8,128)S(1)}, f32[256,2048]{1,0:T(8,128)}, u32[]{:S(2)}) copy-start(f32[256,2048]{1,0:T(8,128)} %param.3) | copy-start | bytes 6291460
  86.6 2.2 copy-start.1
  156.1 0.8 copy-start.4
  272.1 1.3 copy-start.5
  272.9 2.0 copy-start.2
  276.1 2.5 copy-start.3
Sparse Core Ops, SparseCore 0:
  14.3 72.1 all-reduce.3
  93.5 59.2 all-reduce.5
where the time goes:
time: 288 us
  waiting for transfers between devices  130 us (45%)
  other arithmetic  114 us (40%)
  matrix products  16.1 us (6%)
  between operations  14.3 us (5%)
  local copies, waits for them, and re-layouts  13.3 us (5%)
    psum x1, waiting for transfers between devices, body(): pivot_rows = lax.psum(picked, 'wave')  70.8 us
    another operation x10, other arithmetic, body(): factors = jnp.linalg.cholesky(jnp.stack([gram, node_gram]))  67.8 us
    psum x1, waiting for transfers between devices, body(): total = lax.psum(jnp.dot(left, right.T, precision=HIGH), 'freq')  59.4 us
    another operation x4, other arithmetic, body(): inverses = jax.scipy.linalg.solve_triangular(factors, eye, lower=True)  40.3 us
  transfers between devices with their start and end apart: 2, of which 2 were waited for; matrix products, arithmetic and copies ran while one was open for 0% of the time, Pallas kernels for 0%

commit v1 on v0

--- a/solution.py
+++ b/solution.py
@@ -21,7 +21,7 @@
     weighted = pivot_rows * node_count[None, :]
     left = jnp.concatenate([pivot_rows, waveforms], axis=0)
     right = jnp.concatenate([pivot_rows, weighted], axis=0)
-    total = lax.psum(jnp.dot(left, right.T, precision=HIGH), "freq")
+    total = jnp.sum(lax.all_gather(jnp.dot(left, right.T, precision=HIGH), "freq"), axis=0)
     gram, node_gram = (total[:count, :count], total[:count, count:])
     cross, node_cross = (total[count:, :count], total[count:, count:])
     factors = jnp.linalg.cholesky(jnp.stack([gram, node_gram]))

time: 288 us -> 337 us (1.17)
  waiting for transfers between devices: 130 us -> 150 us
  other arithmetic: 114 us -> 131 us
  local copies, waits for them, and re-layouts: 13.3 us -> 20.7 us
  matrix products: 16.1 us -> 19.9 us
    all_gather x0 -> x1, waiting for transfers between devices: none -> 79.7 us  [body(): lax.all_gather(jnp.dot(left, right.T, precision=HIGH), 'freq')]
    psum x1 -> x0, waiting for transfers between devices: 59.4 us -> none  [body(): total = lax.psum(jnp.dot(left, right.T, precision=HIGH), 'freq')]
    another operation x10, other arithmetic: 67.8 us -> 75.2 us  [body(): factors = jnp.linalg.cholesky(jnp.stack([gram, node_gram]))]
    reduce_sum x0 -> x1, other arithmetic: none -> 4.49 us  [body(): jnp.sum(lax.all_gather(jnp.dot(left, right.T, precision=HIGH), 'freq'), a...]
    another operation x4, other arithmetic: 40.3 us -> 43.9 us  [body(): inverses = jax.scipy.linalg.solve_triangular(factors, eye, lower=True)]
  transfers between devices with their start and end apart: 2 -> 2, of which waited for: 2 -> 2; matrix products, arithmetic and copies ran while one was open for 0% -> 1% of each run, Pallas kernels for 0% -> 0%
where the time goes in v1:
time: 337 us; the launch traced here: 336 us
  waiting for transfers between devices  150 us (45%)
  other arithmetic  131 us (39%)
  local copies, waits for them, and re-layouts  20.7 us (6%)
  matrix products  19.9 us (6%)
  between operations  14.2 us (4%)
    all_gather x1, waiting for transfers between devices, body(): lax.all_gather(jnp.dot(left, right.T, precision=HIGH), 'freq')  79.7 us
    another operation x10, other arithmetic, body(): factors = jnp.linalg.cholesky(jnp.stack([gram, node_gram]))  75.2 us
    psum x1, waiting for transfers between devices, body(): pivot_rows = lax.psum(picked, 'wave')  70.8 us
    another operation x4, other arithmetic, body(): inverses = jax.scipy.linalg.solve_triangular(factors, eye, lower=True)  43.9 us
    another operation x6, local copies, waits for them, and re-layouts  7.18 us
  transfers between devices with their start and end apart: 2, of which 2 were waited for; matrix products, arithmetic and copies ran while one was open for 1% of the time, Pallas kernels for 0%

profile of v1, /device:TPU:0, one launch (start us, length us, event | category | flops | bytes accessed | tf_op | source)
XLA Modules:
  0.0 336.1 jit_solution(15563432875812331794)
XLA Ops:
  8.6 4.0 %gather_fusion = f32[256,2048]{1,0:T(8,128)S(1)} fusion(f32[256,2048]{1,0:T(8,128)} %param.3, s32[1024]{0:T(1024)S(1)} %pad_clamp_fusion), kind=kCustom, calls=%fused_computation | custom fusion | bytes 4195328 | tf_op jit(solution)/shard_map/jit(_take)/gather | solution.py:17
  12.6 1.6 select_multiply_fusion
  15.8 70.8 %all-reduce.3.cloned.1.call-done = f32[256,2048]{1,0:T(8,128)} async-done(((f32[256,2048]{1,0:T(8,128)}), f32[256,2048]{1,0:T(8,128)}) %all-reduce.3.cloned.1.call-update) | async-done | bytes 2097168 | tf_op jit(solution)/shard_map/psum | solution.py:18
  86.6 2.0 broadcast_multiply_fusion
  88.8 4.6 %fusion = f32[512,512]{1,0:T(8,128)} fusion(f32[256,2048]{1,0:T(8,128)S(1)} %copy-done.1, f32[256,2048]{1,0:T(8,128)S(1)} %copy-done, f32[256,2048]{1,0:T(8,128)S(1)} %broadcast_multiply_fusion), kind=kOutput, calls=%fused_computation.6 | convolution fusion | flops 3223322624 | bytes 7340032 | tf_op jit(solution)/shard_map/dot_general | solution.py:24
  95.9 79.7 %all-gather.3.cloned.1.call-done = f32[4096,512]{1,0:T(8,128)} async-done(((f32[512,512]{1,0:T(8,128)}), f32[4096,512]{1,0:T(8,128)}) %all-gather.3.cloned.1.call-update) | async-done | bytes 8388624 | tf_op jit(solution)/shard_map/all_gather | solution.py:24
  175.6 4.5 %reduce_sum.19 = f32[512,512]{1,0:T(8,128)S(1)} reduce(f32[8,512,512]{2,1,0:T(8,128)} %bitcast.59, f32[]{:T(128)} %constant.114.clone.1), dimensions={0}, to_apply=%region_2.3 | reduce | flops 1835008 | bytes 9437188 | tf_op jit(solution)/shard_map/reduce_sum | solution.py:24
  182.0 1.8 copy.34
  183.8 1.8 pad_maximum_fusion.4
  185.6 2.0 copy.22
  189.6 23.6 %custom-call.17 = f32[2,128,128]{2,1,0:T(8,128)S(1)} custom-call(f32[2,128,128]{2,1,0:T(8,128)S(1)} %cholesky.122), custom_call_target="Cholesky" | custom-call | tf_op jit(solution)/shard_map/jit(cholesky)/cholesky | solution.py:27
  215.4 21.1 %custom-call.18 = f32[2,1,128,128]{2,3,1,0:T(8,128)} custom-call(f32[2,1,128,128]{3,2,1,0:T(8,128)} %select_bitcast_fusion), custom_call_target="InvertDiagBlocksLowerTriangular" | custom-call | tf_op jit(solution)/shard_map/jit(cholesky)/cholesky | solution.py:27
  236.6 1.9 constant_dynamic-update-slice_fusion.1
  238.5 2.0 convolution_subtract_fusion.2
  240.4 24.9 %custom-call.19 = f32[2,128,128]{2,1,0:T(8,128)} custom-call(f32[2,128,128]{2,1,0:T(8,128)} %convolution_subtract_fusion.2), custom_call_target="Cholesky" | custom-call | tf_op jit(solution)/shard_map/jit(cholesky)/cholesky | solution.py:27
  265.3 1.6 select_reduce_fusion
  267.1 2.0 select_select_fusion
  269.7 7.2 %while.1 = (s32[]{:T(128)}, f32[2,256,256]{2,1,0:T(8,128)}, s32[2,2]{1,0:T(2,128)S(1)}, f32[2,2,128,128]{3,2,0,1:T(8,128)}, s32[]{:T(128)}) while((s32[]{:T(128)}, f32[2,256,256]{2,1,0:T(8,128)}, s32[2,2]{1,0:T(2,128)S(1)}, f32[2,2,128,128]{3,2,0,1:T(8,128)}, s32[]{:T(128)}) %tuple.30), condition=%wide.while_cond, body=%wide.while_body.sunk | while | flops 2 | bytes 263777 | solution.py:29
  270.3 3.0 bitcast_dynamic-update-slice_fusion.2
  273.9 3.0 bitcast_dynamic-update-slice_fusion.2
  276.9 40.8 %custom-call.20 = f32[2,2,128,128]{2,3,1,0:T(8,128)} custom-call(f32[2,2,128,128]{3,2,1,0:T(8,128)} %bitcast.66), custom_call_target="InvertDiagBlocksLowerTriangular" | custom-call | tf_op jit(solution)/shard_map/jit(_solve_triangular)/vmap()/triangular_solve | solution.py:29
  320.3 1.5 fusion.13
  324.2 2.5 convolution_subtract_fusion
  326.7 2.5 fusion.34
  (50 shorter events, 18.8 us)
Async XLA Ops:
  7.2 79.4 %all-reduce.3.cloned.1.call-start = ((), (), s32[]{:S(2)}) async-start(), calls=%async_computation | async-start | bytes 4194304 | tf_op jit(solution)/shard_map/psum | solution.py:18
  14.2 0.7 copy-start.6
  14.2 161.4 %all-gather.3.cloned.1.call-start = ((), (), s32[]{:S(2)}) async-start(), calls=%async_computation.1 | async-start | bytes 9437184 | tf_op jit(solution)/shard_map/all_gather | solution.py:24
  15.8 72.8 %copy-start = (f32[256,2048]{1,0:T(8,128)S(1)}, f32[256,2048]{1,0:T(8,128)}, u32[]{:S(2)}) copy-start(f32[256,2048]{1,0:T(8,128)} %param.3) | copy-start | bytes 6291460
  86.6 2.2 copy-start.1
  188.8 0.8 copy-start.4
  215.4 102.2 %copy-start.5 = (f32[128,256]{1,0:T(8,128)S(1)}, f32[128,256]{1,0:T(8,128)}, u32[]{:S(2)}) copy-start(f32[128,256]{1,0:T(8,128)} %get-tuple-element.28) | copy-start | bytes 393220
  320.3 2.7 copy-start.2
  324.2 2.5 copy-start.3
Sparse Core Ops, SparseCore 0:
  14.3 72.1 all-reduce.2
  93.5 82.0 all-gather.2
